TPU v7x, 128 devices: a whole 4x4x4 slice. The times are simulated.
128 devices in a mesh: blk: 16 (over z_lo, y, core), seq: 8 (over x, z_hi).
Axes of the slice: x: 4, y: 4, z: 4 (z_hi: 2, z_lo: 2; z = z_hi * 2 + z_lo), core: 2. Of those that a mesh axis runs over, the one named last changes fastest.
Arguments:
- layer_input: bfloat16 [16, 1024, 8192], P('blk', 'seq'), may hold values from -6 to 6
- queries: bfloat16 [16, 1024, 4096], P('blk', 'seq'), may hold values from -48 to 48, as said below
- grad_out: bfloat16 [16, 1024, 4096], P('blk', 'seq'), may hold values from -6 to 6
- segment_ids: int32 [16, 1024], P('blk', 'seq'), may hold values from 0 to 3, never falling along the last dimension, each value on 1 to 512 neighbouring positions
- kv_weight: bfloat16 [8192, 1024], P(('blk', 'seq')), may hold values from -0.0625 to 0.0625
- norm_gain: float32 [8192], replicated, may hold values from 0.5 to 1.5
Outputs:
- attended: bfloat16 [16, 1024, 4096], P('blk', 'seq')
- grad_queries: bfloat16 [16, 1024, 4096], P('blk', 'seq')
- grad_input: bfloat16 [16, 1024, 8192], P('blk', 'seq')
- grad_weight: float32 [8192, 1024], P(('blk', 'seq'))
- grad_gain: float32 [8192], replicated
Inputs may be any that keep to these rules, and one draw needn't show every extreme that they name: Projected queries; some rows may be larger than others.
All inputs are finite; a program needn't handle non-finite values.
Results may differ from a plain program's by a relative error of at most 0.02.
The roundings to bfloat16 on the way count: a program that leaves them out, or rounds other values in their place, can miss the bound.
Values may be sent and summed in bfloat16 or wider, within the bound.
No kernel may reach another device: no remote copies, remote signals or barrier semaphores. Data moves between devices by JAX's collectives and lax.ppermute only.
A program may use at most 128 MiB of HBM per device.

v0:
```python
import jax
import jax.numpy as jnp
from jax import lax
from jax.sharding import PartitionSpec as P

HEAD = 128
epsilon = 1e-05


def cut_along(shard, dim, length):
    lengths = shard.shape
    pieces = shard.reshape(*lengths[:dim], length, lengths[dim] // length, *lengths[dim + 1 :])
    return jnp.moveaxis(pieces, dim, 0)


def sum_at_owner(shard, axis, dim):
    length = lax.axis_size(axis)
    pieces = lax.all_to_all(cut_along(shard, dim, length), axis, 0, 0, tiled=True)
    return jnp.sum(pieces, axis=0)


def shards(layer_input, queries, grad_out, segment_ids, kv_weight, norm_gain):
    f32 = jnp.float32
    tok_rows = layer_input.shape[1]
    model_width = layer_input.shape[2]
    seq_devices = lax.axis_size("seq")
    blk_devices = lax.axis_size("blk")
    length = tok_rows * seq_devices
    seq_index = lax.axis_index("seq")
    kv_total = kv_weight.shape[1]
    kv_width = kv_total // 2
    kv_heads = kv_width // HEAD
    query_count = queries.shape[2] // HEAD
    group_size = query_count // kv_heads
    score_scale = HEAD ** (-0.5)
    piece_cols = kv_weight.shape[0]
    source = layer_input[0].astype(f32)
    inv_rms = lax.rsqrt(jnp.mean(source * source, axis=1, keepdims=True) + epsilon)
    scaled = source * inv_rms
    normed = (scaled * norm_gain).astype(jnp.bfloat16)
    split_cols = normed.reshape(tok_rows, blk_devices, seq_devices, piece_cols)
    columns = lax.all_to_all(split_cols, "seq", split_axis=2, concat_axis=0, tiled=True).reshape(
        length, blk_devices * piece_cols
    )
    weight_slab = lax.all_gather(kv_weight, "blk", axis=0, tiled=True)
    query_heads = queries[0].reshape(tok_rows, kv_heads, group_size, HEAD)
    query_pos = seq_index * tok_rows + jnp.arange(tok_rows, dtype=jnp.int32)
    query_doc = segment_ids[0]
    grad_heads = grad_out[0].reshape(tok_rows, kv_heads, group_size, HEAD).transpose(1, 2, 0, 3)

    def scores_of(kv_piece, doc_piece):
        rows_here = kv_piece.shape[0]
        key_heads = kv_piece[:, :kv_width].reshape(rows_here, kv_heads, HEAD)
        raw_scores = (
            jnp.einsum("qgjd,kgd->gjqk", query_heads, key_heads, preferred_element_type=f32)
            * score_scale
        )
        key_pos = jnp.arange(rows_here, dtype=jnp.int32)
        allowed = (key_pos[None, :] <= query_pos[:, None]) & (
            doc_piece[None, :] == query_doc[:, None]
        )
        return (jnp.where(allowed, raw_scores, -1e30), allowed, key_heads)

    stat_shape = (kv_heads, group_size, tok_rows, 1)
    kv_own = sum_at_owner(
        jnp.dot(columns, weight_slab, preferred_element_type=f32), "seq", 0
    ).astype(jnp.bfloat16)
    row_max = jnp.full(stat_shape, -1e30, f32)
    kv_piece = lax.all_gather(kv_own, "seq", axis=0, tiled=True)
    doc_piece = lax.all_gather(query_doc, "seq", axis=0, tiled=True)
    rows_here = kv_piece.shape[0]
    masked, allowed, key_heads = scores_of(kv_piece, doc_piece)
    new_max = jnp.maximum(row_max, jnp.max(masked, axis=-1, keepdims=True))
    expo_terms = jnp.where(allowed, jnp.exp(masked - new_max), 0.0)
    value_heads = kv_piece[:, kv_width:].reshape(rows_here, kv_heads, HEAD)
    weights = expo_terms.astype(jnp.bfloat16)
    weighted = jnp.einsum("gjqk,kgd->gjqd", weights, value_heads, preferred_element_type=f32)
    row_sum = jnp.sum(expo_terms, axis=-1, keepdims=True)
    row_max, row_sum, weighted = (new_max, row_sum, weighted)
    summed = weighted / row_sum
    attended = (
        summed.transpose(2, 0, 1, 3).reshape(tok_rows, query_count * HEAD).astype(jnp.bfloat16)
    )
    log_total = row_max + jnp.log(row_sum)
    attended_heads = attended.reshape(tok_rows, kv_heads, group_size, HEAD).transpose(1, 2, 0, 3)
    row_delta = jnp.sum(grad_heads.astype(f32) * attended_heads.astype(f32), axis=-1, keepdims=True)
    kv_piece = lax.all_gather(kv_own, "seq", axis=0, tiled=True)
    doc_piece = lax.all_gather(query_doc, "seq", axis=0, tiled=True)
    rows_here = kv_piece.shape[0]
    masked, allowed, key_heads = scores_of(kv_piece, doc_piece)
    softmax_probs = jnp.where(allowed, jnp.exp(masked - log_total), 0.0)
    value_heads = kv_piece[:, kv_width:].reshape(rows_here, kv_heads, HEAD)
    grad_probs = jnp.einsum("gjqd,kgd->gjqk", grad_heads, value_heads, preferred_element_type=f32)
    grad_scores = (softmax_probs * (grad_probs - row_delta)).astype(jnp.bfloat16)
    probs_half = softmax_probs.astype(jnp.bfloat16)
    grad_values = jnp.einsum("gjqk,gjqd->kgd", probs_half, grad_heads, preferred_element_type=f32)
    grad_keys = (
        jnp.einsum("gjqk,qgjd->kgd", grad_scores, query_heads, preferred_element_type=f32)
        * score_scale
    )
    grad_query = (
        jnp.einsum("gjqk,kgd->qgjd", grad_scores, key_heads, preferred_element_type=f32)
        * score_scale
    )
    new_rows = jnp.concatenate(
        [grad_keys.reshape(rows_here, kv_width), grad_values.reshape(rows_here, kv_width)], axis=1
    )
    grad_rows = new_rows
    grad_query, grad_rows = (grad_query, grad_rows)
    grad_own = sum_at_owner(grad_rows, "seq", 0).astype(jnp.bfloat16)
    grad_kv = lax.all_gather(grad_own, "seq", axis=0, tiled=True)
    grad_queries = grad_query.reshape(tok_rows, query_count * HEAD).astype(jnp.bfloat16)
    slab_back = lax.all_gather(kv_weight, "blk", axis=0, tiled=True)
    grad_weight = lax.psum_scatter(
        lax.dot_general(columns, grad_kv, (((0,), (0,)), ((), ())), preferred_element_type=f32),
        "blk",
        scatter_dimension=0,
        tiled=True,
    )
    grad_cols = lax.dot_general(
        grad_kv, slab_back, (((1,), (1,)), ((), ())), preferred_element_type=f32
    ).astype(jnp.bfloat16)
    grad_cols = grad_cols.reshape(length, blk_devices, 1, piece_cols)
    grad_normed = lax.all_to_all(grad_cols, "seq", split_axis=0, concat_axis=2, tiled=True).reshape(
        tok_rows, model_width
    )
    grad_norm = grad_normed.astype(f32)
    grad_gain = lax.psum(jnp.sum(grad_norm * scaled, axis=0), ("blk", "seq"))
    grad_hat = grad_norm * norm_gain
    grad_input = inv_rms * (grad_hat - scaled * jnp.mean(grad_hat * scaled, axis=1, keepdims=True))
    return (
        attended[None],
        grad_queries[None],
        grad_input.astype(jnp.bfloat16)[None],
        grad_weight,
        grad_gain,
    )


def solution(mesh):
    in_specs = (
        P("blk", "seq", None),
        P("blk", "seq", None),
        P("blk", "seq", None),
        P("blk", "seq"),
        P(("blk", "seq"), None),
        P(),
    )
    out_specs = (
        P("blk", "seq", None),
        P("blk", "seq", None),
        P("blk", "seq", None),
        P(("blk", "seq"), None),
        P(),
    )
    return jax.shard_map(shards, mesh=mesh, in_specs=in_specs, out_specs=out_specs, check_vma=False)
```

profile of v0, /device:TPU:1, one launch (start us, length us, event | category | flops | bytes accessed | tf_op | source)
XLA Modules:
  0.0 534.6 jit_solution(473694179402004484)
XLA Ops:
  17.7 38.3 %all_to_all.34 = bf16[128,16,8,64]{0,3,1,2:T(8,128)(2,1)} all-to-all(bf16[128,16,8,64]{0,3,1,2:T(8,128)(2,1)S(1)} %copy.149), channel_id=1, replica_groups=mesh['blk'=16,'seq'=8] {'seq'}, dimensions={2} | all-to-all | bytes 4194304 | tf_op jit(solution)/shard_map/all_to_all | solution.py:42
  56.0 8.3 %all-gather.5.cloned.1.call-done = bf16[1024,1024]{1,0:T(8,128)(2,1)} async-done(((bf16[64,1024]{1,0:T(8,128)(2,1)}), bf16[1024,1024]{1,0:T(8,128)(2,1)}) %all-gather.5.cloned.1.call-update) | async-done | bytes 2097168 | tf_op jit(solution)/shard_map/all_gather | solution.py:45
  68.9 55.1 %all_to_all.35 = f32[8,128,1024]{2,1,0:T(8,128)} all-to-all(f32[8,128,1024]{2,1,0:T(8,128)S(1)} %fusion.22), channel_id=1, replica_groups=mesh['blk'=16,'seq'=8] {'seq'}, dimensions={0} | all-to-all | bytes 8388608 | tf_op jit(solution)/shard_map/all_to_all | solution.py:18
  131.0 17.1 %all-gather = s32[1,1024]{1,0:T(1,128)S(1)} all-gather(s32[1,128]{1,0:T(1,128)S(1)} %copy-done.8), channel_id=2, replica_groups=mesh['blk'=16,'seq'=8] {'seq'}, dimensions={1}, use_global_device_ids=true | all-gather | bytes 4608 | tf_op jit(solution)/shard_map/all_gather | solution.py:70
  148.4 30.2 %all-gather.7.cloned.1.call-done = bf16[1024,1024]{1,0:T(8,128)(2,1)} async-done(((bf16[128,1024]{1,0:T(8,128)(2,1)}), bf16[1024,1024]{1,0:T(8,128)(2,1)}) %all-gather.7.cloned.1.call-update) | async-done | bytes 2097168 | tf_op jit(solution)/shard_map/all_gather | solution.py:69
  183.0 9.1 %fusion.33 = (f32[4,8,128]{2,1,0:T(8,128)S(1)}, f32[4,8,128,1024]{2,3,1,0:T(8,128)}) fusion(bf16[1024,4,128,1]{0,2,3,1:T(8,128)(2,1)S(1)} %bitcast.122, bf16[128,4,8,128]{3,2,1,0:T(8,128)(2,1)} %bitcast.124, pred[128,1024]{0,1:T(8,128)(4,1)S(1)} %fusion.29), kind=kOutput, calls=%fused_computation.52 | convolution fusion | flops 1086320640 | bytes 19021824 | tf_op jit(solution)/shard_map/qgjd,kgd->gjqk/dot_general | solution.py:55
  194.4 8.7 %fusion.1 = f32[4,8,128]{2,1,0:T(8,128)S(1)} fusion(f32[4,8,128,1024]{2,3,1,0:T(8,128)} %get-tuple-element.45, f32[4,8,128]{2,1,0:T(8,128)S(1)} %broadcast_maximum_fusion, pred[128,1024]{0,1:T(8,128)(4,1)S(1)} %fusion.29), kind=kLoop, calls=%fused_computation.5 | loop fusion | flops 12578816 | bytes 16941056 | tf_op jit(solution)/shard_map/reduce_sum | solution.py:78
  203.1 9.9 %fusion.21 = (bf16[128,4,8,128]{0,3,2,1:T(8,128)(2,1)}, f32[4,8,128,128]{2,3,1,0:T(8,128)S(1)}) fusion(f32[128,4,8]{0,2,1:T(8,128)S(1)} %bitcast.140, bf16[1024,4,128,1]{0,2,3,1:T(8,128)(2,1)S(1)} %bitcast.138, f32[4,8,128,1024]{2,3,1,0:T(8,128)} %get-tuple-element.45, f32[4,8,128]{2,1,0:T(8,128)S(1)} %broadcast_maximum_fusion, ...), kind=kOutput, calls=%fused_computation.32 | convolution fusion | flops 1087373312 | bytes 21135360 | tf_op jit(solution)/shard_map/gjqk,kgd->gjqd/dot_general | solution.py:77
  213.4 9.5 %fusion.24 = f32[1024,4,128]{2,0,1:T(8,128)} fusion(bf16[4,8,128,128]{2,3,1,0:T(8,128)(2,1)S(1)} %bitcast.131, f32[4,8,128,1024]{2,3,1,0:T(8,128)} %get-tuple-element.45, f32[4,8,128]{2,1,0:T(8,128)S(1)} %log_add_fusion, pred[128,1024]{0,1:T(8,128)(4,1)S(1)} %fusion.29), kind=kOutput, calls=%fused_computation.39 | convolution fusion | flops 1086324736 | bytes 20070400 | tf_op jit(solution)/shard_map/gjqk,gjqd->kgd/dot_general | solution.py:96
  222.9 10.9 %fusion = bf16[4,8,128,1024]{2,3,1,0:T(8,128)(2,1)} fusion(f32[4,8,128,1024]{2,3,1,0:T(8,128)} %get-tuple-element.45, bf16[1024,4,128,1]{0,2,3,1:T(8,128)(2,1)S(1)} %bitcast.139, bf16[4,8,128,128]{2,3,1,0:T(8,128)(2,1)S(1)} %bitcast.132, f32[4,8,128]{2,1,0:T(8,128)S(1)} %multiply_reduce_fusion.3, f32[4,8,128]{2,1,0:T(8,128)S(1)} %log_add_fusion, ...), kind=kOutput, calls=%fused_computation.1 | convolution fusion | flops 1094713344 | bytes 27426816 | tf_op jit(solution)/shard_map/gjqd,kgd->gjqk/dot_general | solution.py:93
  240.2 7.1 %fusion.20 = f32[1024,4,128]{2,0,1:T(8,128)} fusion(bf16[4,8,128,1024]{2,3,1,0:T(8,128)(2,1)} %fusion, bf16[128,4,8,128]{3,2,1,0:T(8,128)(2,1)S(1)} %bitcast.125), kind=kOutput, calls=%fused_computation.30 | convolution fusion | flops 1074266112 | bytes 11534336 | tf_op jit(solution)/shard_map/gjqk,qgjd->kgd/dot_general | solution.py:98
  253.5 50.9 %all_to_all.36 = f32[8,128,1024]{1,2,0:T(8,128)} all-to-all(f32[8,128,1024]{1,2,0:T(8,128)S(1)} %copy.164), channel_id=1, replica_groups=mesh['blk'=16,'seq'=8] {'seq'}, dimensions={0} | all-to-all | bytes 8388608 | tf_op jit(solution)/shard_map/all_to_all | solution.py:18
  307.8 4.7 copy.171
  312.5 51.4 %all-gather.9.cloned.1.call-done = bf16[1024,1024]{0,1:T(8,128)(2,1)} async-done(((bf16[128,1024]{0,1:T(8,128)(2,1)}), bf16[1024,1024]{0,1:T(8,128)(2,1)}) %all-gather.9.cloned.1.call-update) | async-done | bytes 2097168 | tf_op jit(solution)/shard_map/all_gather | solution.py:111
  363.9 6.5 %fusion.17 = f32[1024,1024]{1,0:T(8,128)} fusion(bf16[1024,1024]{0,1:T(8,128)(2,1)} %all-gather.9.cloned.1.call-done, bf16[128,8,8,128]{3,2,1,0:T(8,128)(2,1)} %bitcast.135), kind=kOutput, calls=%fused_computation.26 | convolution fusion | flops 2147483648 | bytes 8388608 | tf_op jit(solution)/shard_map/dot_general | solution.py:115
  370.4 5.9 %convolution_convert_fusion = bf16[1024,1024]{0,1:T(8,128)(2,1)} fusion(bf16[1024,1024]{1,0:T(8,128)(2,1)} %all-gather.5.cloned.1.call-done, bf16[1024,1024]{0,1:T(8,128)(2,1)} %all-gather.9.cloned.1.call-done), kind=kOutput, calls=%fused_computation.38 | convolution fusion | flops 2148532224 | bytes 6291456 | tf_op jit(solution)/shard_map/dot_general | solution.py:120
  376.3 6.2 %copy.166 = bf16[1024,16,1,64]{3,1,2,0:T(8,128)(2,1)} copy(bf16[1024,16,1,64]{0,3,1,2:T(8,128)(2,1)} %bitcast.134) | data formatting | bytes 4194304 | tf_op jit(solution)/shard_map/reshape | solution.py:123
  382.5 7.6 %reshape.223 = bf16[8,2,65536]{2,1,0:T(2,128)(2,1)} reshape(bf16[1024,1,16,64]{3,2,1,0:T(8,128)(2,1)} %bitcast.119) | data formatting | bytes 4194304
  397.9 5.6 %multiply_convert_fusion.1 = bf16[4,128,8,128]{3,1,2,0:T(8,128)(2,1)} fusion(bf16[1024,4,128,1]{0,2,3,1:T(8,128)(2,1)S(1)} %bitcast.123, bf16[4,8,128,1024]{2,3,1,0:T(8,128)(2,1)} %fusion), kind=kOutput, calls=%fused_computation.35 | convolution fusion | flops 1074790400 | bytes 10485760 | tf_op jit(solution)/shard_map/gjqk,kgd->qgjd/dot_general | solution.py:102
  405.9 22.6 %all-to-all-done.3 = bf16[8,2,65536]{2,1,0:T(2,128)(2,1)} async-done(((bf16[8,2,65536]{2,1,0:T(2,128)(2,1)}), bf16[8,2,65536]{2,1,0:T(2,128)(2,1)}, u32[]{:S(2)}, u32[]{:S(2)}) %all-to-all-start.3) | async-done | bytes 2097184 | tf_op jit(solution)/shard_map/all_to_all | solution.py:124
  428.4 7.4 %reshape.224 = bf16[1024,1,16,64]{3,2,1,0:T(8,128)(2,1)} reshape(bf16[8,2,65536]{2,1,0:T(2,128)(2,1)} %all-to-all-done.3) | data formatting | bytes 4194304
  435.8 5.5 %copy.167 = bf16[1024,16,1,64]{0,3,2,1:T(8,128)(2,1)} copy(bf16[1024,16,1,64]{3,1,2,0:T(8,128)(2,1)} %bitcast.120) | data formatting | bytes 4194304 | tf_op jit(solution)/shard_map/all_to_all | solution.py:124
  446.7 4.8 multiply_reduce_fusion
  460.2 67.6 %psum.7 = f32[8192]{0:T(1024)} all-reduce(f32[8192]{0:T(1024)S(1)} %reduce_sum.72), channel_id=1, replica_groups=mesh['blk'=16,'seq'=8] {'blk','seq'}, use_global_device_ids=true, to_apply=%region_9.10 | all-reduce | flops 8192 | bytes 65536 | tf_op jit(solution)/shard_map/psum | solution.py:128
  (65 shorter events, 69.7 us)
Async XLA Ops:
  7.2 57.1 %all-gather.5.cloned.1.call-start = ((), (), s32[]{:S(2)}) async-start(), calls=%async_computation.5 | async-start | bytes 2228224 | tf_op jit(solution)/shard_map/all_gather | solution.py:45
  7.9 5.5 %copy-start.7 = (f32[8192]{0:T(1024)S(1)}, f32[8192]{0:T(1024)}, u32[]{:S(2)}) copy-start(f32[8192]{0:T(1024)} %param.11) | copy-start | bytes 98308
  7.9 170.6 %all-gather.7.cloned.1.call-start = ((), (), s32[]{:S(2)}) async-start(), calls=%async_computation.6 | async-start | bytes 2359296 | tf_op jit(solution)/shard_map/all_gather | solution.py:69
  124.0 3.5 copy-start.5
  124.0 7.0 %copy-start.8 = (s32[1,128]{1,0:T(1,128)S(1)}, s32[1,128]{1,0:T(1,128)}, u32[]{:S(2)}) copy-start(s32[1,128]{1,0:T(1,128)} %param.9) | copy-start | bytes 1540
  127.5 236.4 %all-gather.9.cloned.1.call-start = ((), (), s32[]{:S(2)}) async-start(), calls=%async_computation.7 | async-start | bytes 2359296 | tf_op jit(solution)/shard_map/all_gather | solution.py:111
  194.4 8.7 %copy-start.6 = (bf16[1024,512]{0,1:T(8,128)(2,1)S(1)}, bf16[1024,512]{0,1:T(8,128)(2,1)}, u32[]{:S(2)}) copy-start(bf16[1024,512]{0,1:T(8,128)(2,1)} %copy.154) | copy-start | bytes 3145732
  203.1 9.9 %copy-start.3 = (bf16[1,128,4096]{1,2,0:T(8,128)(2,1)S(1)}, bf16[1,128,4096]{1,2,0:T(8,128)(2,1)}, u32[]{:S(2)}) copy-start(bf16[1,128,4096]{1,2,0:T(8,128)(2,1)} %copy.156) | copy-start | bytes 3145732
  236.7 3.5 copy-start.1
  250.2 2.2 copy-start.2
  307.6 220.3 %reduce-scatter.2.cloned.1.call-start = ((), (), s32[]{:S(2)}) async-start(), calls=%async_computation.8 | async-start | bytes 4456448 | tf_op jit(solution)/shard_map/reduce_scatter | solution.py:114
  390.1 38.4 %all-to-all-start.3 = ((bf16[8,2,65536]{2,1,0:T(2,128)(2,1)}), bf16[8,2,65536]{2,1,0:T(2,128)(2,1)}, u32[]{:S(2)}, u32[]{:S(2)}) async-start(bf16[8,2,65536]{2,1,0:T(2,128)(2,1)} %reshape.223), calls=%async_computation.3 | async-start | bytes 4194304 | tf_op jit(solution)/shard_map/all_to_all | solution.py:124
  444.4 2.2 copy-start
  444.4 2.3 copy-start.4
Sparse Core Ops, SparseCore 0:
  9.7 54.5 all-gather.4
  127.6 50.8 all-gather.6
  307.7 56.0 all-gather.8
  370.5 72.2 reduce-scatter.1
where the time goes:
time: 540 us; the launch traced here: 535 us
  blocking collectives  229 us (42%)
  waiting for transfers between devices  113 us (21%)
  local copies, waits for them, and re-layouts  70.6 us (13%)
  matrix products  69.1 us (13%)
  other arithmetic  33.7 us (6%)
  between operations  14.2 us (3%)
    all_to_all x2, blocking collectives, sum_at_owner(): lax.all_to_all(cut_along(shard, dim, length), axis, 0, 0, tiled=True)  106 us
    psum x1, blocking collectives, shards(): grad_gain = lax.psum(jnp.sum(grad_norm * scaled, axis=0), ('blk', 'seq'))  67.6 us
    all_gather x1, waiting for transfers between devices, shards(): grad_kv = lax.all_gather(grad_own, 'seq', axis=0, tiled=True)  51.4 us
    unnamed x29, local copies, waits for them, and re-layouts  38.6 us
    all_to_all x1, blocking collectives, shards(): lax.all_to_all(split_cols, 'seq', split_axis=2, concat_axis=0, tiled=True)  38.3 us
    all_gather x1, waiting for transfers between devices, shards(): kv_piece = lax.all_gather(kv_own, 'seq', axis=0, tiled=True)  30.2 us
    all_to_all x1, waiting for transfers between devices, shards(): lax.all_to_all(grad_cols, 'seq', split_axis=0, concat_axis=2, tiled=True)  22.6 us
    all_gather x1, blocking collectives, shards(): doc_piece = lax.all_gather(query_doc, 'seq', axis=0, tiled=True)  17.1 us
  transfers between devices with their start and end apart: 5, of which 4 were waited for; matrix products, arithmetic and copies ran while one was open for 15% of the time, Pallas kernels for 0%

commit v1 on v0

--- a/solution.py
+++ b/solution.py
@@ -5,6 +5,12 @@
 
 HEAD = 128
 epsilon = 1e-05
+
+
+def summed_here(x, axis):
+    blocks = lax.all_gather(x, axis, axis=0, tiled=False)
+    result = blocks.sum(axis=0)
+    return result
 
 
 def cut_along(shard, dim, length):
@@ -125,7 +131,7 @@
         tok_rows, model_width
     )
     grad_norm = grad_normed.astype(f32)
-    grad_gain = lax.psum(jnp.sum(grad_norm * scaled, axis=0), ("blk", "seq"))
+    grad_gain = summed_here(jnp.sum(grad_norm * scaled, axis=0), ("blk", "seq"))
     grad_hat = grad_norm * norm_gain
     grad_input = inv_rms * (grad_hat - scaled * jnp.mean(grad_hat * scaled, axis=1, keepdims=True))
     return (

time: 540 us -> 829 us (1.54)
  waiting for transfers between devices: 113 us -> 459 us
  blocking collectives: 229 us -> 161 us
    all_gather x0 -> x1, waiting for transfers between devices: none -> 273 us  [summed_here(): blocks = lax.all_gather(x, axis, axis=0, tiled=False)]
    psum x1 -> x0, blocking collectives: 67.6 us -> none  [shards(): grad_gain = lax.psum(jnp.sum(grad_norm * scaled, axis=0), ('blk', 'seq'))]
    reduce_scatter x1, waiting for transfers between devices: 0.01 us -> 61.7 us  [shards(): lax.psum_scatter(lax.dot_general(columns, grad_kv, (((0,), (0,)), ((), ()...]
    unnamed x29 -> x34, local copies, waits for them, and re-layouts: 38.6 us -> 40.2 us
  transfers between devices with their start and end apart: 5 -> 6, of which waited for: 4 -> 6; matrix products, arithmetic and copies ran while one was open for 15% -> 6% of each run, Pallas kernels for 0% -> 0%
where the time goes in v1:
time: 829 us; the launch traced here: 820 us
  waiting for transfers between devices  459 us (55%)
  blocking collectives  161 us (19%)
  local copies, waits for them, and re-layouts  74.1 us (9%)
  matrix products  66.9 us (8%)
  other arithmetic  39.6 us (5%)
  between operations  14.2 us (2%)
    all_gather x1, waiting for transfers between devices, summed_here(): blocks = lax.all_gather(x, axis, axis=0, tiled=False)  273 us
    all_to_all x2, blocking collectives, sum_at_owner(): lax.all_to_all(cut_along(shard, dim, length), axis, 0, 0, tiled=True)  106 us
    reduce_scatter x1, waiting for transfers between devices, shards(): lax.psum_scatter(lax.dot_general(columns, grad_kv, (((0,), (0,)), ((), ()...  61.7 us
    all_gather x1, waiting for transfers between devices, shards(): grad_kv = lax.all_gather(grad_own, 'seq', axis=0, tiled=True)  56.5 us
    unnamed x34, local copies, waits for them, and re-layouts  40.2 us
    all_to_all x1, blocking collectives, shards(): lax.all_to_all(split_cols, 'seq', split_axis=2, concat_axis=0, tiled=True)  38.2 us
    all_gather x1, waiting for transfers between devices, shards(): kv_piece = lax.all_gather(kv_own, 'seq', axis=0, tiled=True)  30.1 us
    all_to_all x1, waiting for transfers between devices, shards(): lax.all_to_all(grad_cols, 'seq', split_axis=0, concat_axis=2, tiled=True)  28 us
  transfers between devices with their start and end apart: 6, of which 6 were waited for; matrix products, arithmetic and copies ran while one was open for 6% of the time, Pallas kernels for 0%

profile of v1, /device:TPU:1, one launch (start us, length us, event | category | flops | bytes accessed | tf_op | source)
XLA Modules:
  0.0 819.7 jit_solution(4407386213503237085)
XLA Ops:
  17.7 38.2 %all_to_all.34 = bf16[128,16,8,64]{0,3,1,2:T(8,128)(2,1)} all-to-all(bf16[128,16,8,64]{0,3,1,2:T(8,128)(2,1)S(1)} %copy.149), channel_id=1, replica_groups=mesh['blk'=16,'seq'=8] {'seq'}, dimensions={2} | all-to-all | bytes 4194304 | tf_op jit(solution)/shard_map/all_to_all | solution.py:48
  55.9 8.4 %all-gather.7.cloned.1.call-done = bf16[1024,1024]{1,0:T(8,128)(2,1)} async-done(((bf16[64,1024]{1,0:T(8,128)(2,1)}), bf16[1024,1024]{1,0:T(8,128)(2,1)}) %all-gather.7.cloned.1.call-update) | async-done | bytes 2097168 | tf_op jit(solution)/shard_map/all_gather | solution.py:51
  69.0 55.1 %all_to_all.35 = f32[8,128,1024]{2,1,0:T(8,128)} all-to-all(f32[8,128,1024]{2,1,0:T(8,128)S(1)} %fusion.22), channel_id=1, replica_groups=mesh['blk'=16,'seq'=8] {'seq'}, dimensions={0} | all-to-all | bytes 8388608 | tf_op jit(solution)/shard_map/all_to_all | solution.py:24
  131.1 17.1 %all-gather = s32[1,1024]{1,0:T(1,128)S(1)} all-gather(s32[1,128]{1,0:T(1,128)S(1)} %copy-done.9), channel_id=2, replica_groups=mesh['blk'=16,'seq'=8] {'seq'}, dimensions={1}, use_global_device_ids=true | all-gather | bytes 4608 | tf_op jit(solution)/shard_map/all_gather | solution.py:76
  148.4 30.1 %all-gather.9.cloned.1.call-done = bf16[1024,1024]{1,0:T(8,128)(2,1)} async-done(((bf16[128,1024]{1,0:T(8,128)(2,1)}), bf16[1024,1024]{1,0:T(8,128)(2,1)}) %all-gather.9.cloned.1.call-update) | async-done | bytes 2097168 | tf_op jit(solution)/shard_map/all_gather | solution.py:75
  183.0 9.1 %fusion.33 = (f32[4,8,128]{2,1,0:T(8,128)S(1)}, f32[4,8,128,1024]{2,3,1,0:T(8,128)}) fusion(bf16[1024,4,128,1]{0,2,3,1:T(8,128)(2,1)S(1)} %bitcast.122, bf16[128,4,8,128]{3,2,1,0:T(8,128)(2,1)} %bitcast.124, pred[128,1024]{0,1:T(8,128)(4,1)S(1)} %fusion.29), kind=kOutput, calls=%fused_computation.52 | convolution fusion | flops 1086320640 | bytes 19021824 | tf_op jit(solution)/shard_map/qgjd,kgd->gjqk/dot_general | solution.py:61
  194.4 8.7 %fusion.1 = f32[4,8,128]{2,1,0:T(8,128)S(1)} fusion(f32[4,8,128,1024]{2,3,1,0:T(8,128)} %get-tuple-element.45, f32[4,8,128]{2,1,0:T(8,128)S(1)} %broadcast_maximum_fusion, pred[128,1024]{0,1:T(8,128)(4,1)S(1)} %fusion.29), kind=kLoop, calls=%fused_computation.5 | loop fusion | flops 12578816 | bytes 16941056 | tf_op jit(solution)/shard_map/reduce_sum | solution.py:84
  203.1 9.9 %fusion.21 = (bf16[128,4,8,128]{0,3,2,1:T(8,128)(2,1)}, f32[4,8,128,128]{2,3,1,0:T(8,128)S(1)}) fusion(f32[128,4,8]{0,2,1:T(8,128)S(1)} %bitcast.140, bf16[1024,4,128,1]{0,2,3,1:T(8,128)(2,1)S(1)} %bitcast.138, f32[4,8,128,1024]{2,3,1,0:T(8,128)} %get-tuple-element.45, f32[4,8,128]{2,1,0:T(8,128)S(1)} %broadcast_maximum_fusion, ...), kind=kOutput, calls=%fused_computation.32 | convolution fusion | flops 1087373312 | bytes 21135360 | tf_op jit(solution)/shard_map/gjqk,kgd->gjqd/dot_general | solution.py:83
  213.4 9.5 %fusion.24 = f32[1024,4,128]{2,0,1:T(8,128)} fusion(bf16[4,8,128,128]{2,3,1,0:T(8,128)(2,1)S(1)} %bitcast.131, f32[4,8,128,1024]{2,3,1,0:T(8,128)} %get-tuple-element.45, f32[4,8,128]{2,1,0:T(8,128)S(1)} %log_add_fusion, pred[128,1024]{0,1:T(8,128)(4,1)S(1)} %fusion.29), kind=kOutput, calls=%fused_computation.39 | convolution fusion | flops 1086324736 | bytes 20070400 | tf_op jit(solution)/shard_map/gjqk,gjqd->kgd/dot_general | solution.py:102
  222.9 10.9 %fusion = bf16[4,8,128,1024]{2,3,1,0:T(8,128)(2,1)} fusion(f32[4,8,128,1024]{2,3,1,0:T(8,128)} %get-tuple-element.45, bf16[1024,4,128,1]{0,2,3,1:T(8,128)(2,1)S(1)} %bitcast.139, bf16[4,8,128,128]{2,3,1,0:T(8,128)(2,1)S(1)} %bitcast.132, f32[4,8,128]{2,1,0:T(8,128)S(1)} %multiply_reduce_fusion.3, f32[4,8,128]{2,1,0:T(8,128)S(1)} %log_add_fusion, ...), kind=kOutput, calls=%fused_computation.1 | convolution fusion | flops 1094713344 | bytes 27426816 | tf_op jit(solution)/shard_map/gjqd,kgd->gjqk/dot_general | solution.py:99
  240.2 7.1 fusion.20
  253.5 50.9 %all_to_all.36 = f32[8,128,1024]{1,2,0:T(8,128)} all-to-all(f32[8,128,1024]{1,2,0:T(8,128)S(1)} %copy.164), channel_id=1, replica_groups=mesh['blk'=16,'seq'=8] {'seq'}, dimensions={0} | all-to-all | bytes 8388608 | tf_op jit(solution)/shard_map/all_to_all | solution.py:24
  307.6 56.5 %all-gather.11.cloned.1.call-done = bf16[1024,1024]{0,1:T(8,128)(2,1)} async-done(((bf16[128,1024]{0,1:T(8,128)(2,1)}), bf16[1024,1024]{0,1:T(8,128)(2,1)}) %all-gather.11.cloned.1.call-update) | async-done | bytes 2097168 | tf_op jit(solution)/shard_map/all_gather | solution.py:117
  364.1 5.9 convolution_convert_fusion
  370.0 6.2 copy.166
  376.2 7.6 reshape.227
  389.1 28.0 %all-to-all-done.3 = bf16[8,2,65536]{2,1,0:T(2,128)(2,1)} async-done(((bf16[8,2,65536]{2,1,0:T(2,128)(2,1)}), bf16[8,2,65536]{2,1,0:T(2,128)(2,1)}, u32[]{:S(2)}, u32[]{:S(2)}) %all-to-all-start.3) | async-done | bytes 2097184 | tf_op jit(solution)/shard_map/all_to_all | solution.py:130
  417.1 7.5 reshape.228
  424.7 5.4 copy.167
  435.3 5.6 multiply_reduce_fusion
  453.3 5.7 multiply_convert_fusion.1
  472.6 273.5 %all-gather.13.cloned.1.call-done = f32[128,1,8192]{2,1,0:T(1,128)} async-done(((f32[1,1,8192]{2,1,0:T(1,128)}), f32[128,1,8192]{2,1,0:T(1,128)}) %all-gather.13.cloned.1.call-update) | async-done | bytes 4194320 | tf_op jit(solution)/shard_map/all_gather | solution.py:11
  746.0 5.2 reduce_sum.79
  751.2 61.7 %reduce-scatter.2.cloned.1.call-done = f32[64,1024]{1,0:T(8,128)} async-done(((f32[1024,1024]{1,0:T(8,128)}), f32[64,1024]{1,0:T(8,128)}) %reduce-scatter.2.cloned.1.call-update) | async-done | bytes 262160 | tf_op jit(solution)/shard_map/reduce_scatter | solution.py:120
  (72 shorter events, 81.8 us)
Async XLA Ops:
  7.2 57.2 %all-gather.7.cloned.1.call-start = ((), (), s32[]{:S(2)}) async-start(), calls=%async_computation.5 | async-start | bytes 2228224 | tf_op jit(solution)/shard_map/all_gather | solution.py:51
  7.9 5.5 copy-start.8
  7.9 170.6 %all-gather.9.cloned.1.call-start = ((), (), s32[]{:S(2)}) async-start(), calls=%async_computation.6 | async-start | bytes 2359296 | tf_op jit(solution)/shard_map/all_gather | solution.py:75
  124.1 3.5 copy-start.6
  124.1 7.0 copy-start.9
  127.6 236.6 %all-gather.11.cloned.1.call-start = ((), (), s32[]{:S(2)}) async-start(), calls=%async_computation.7 | async-start | bytes 2359296 | tf_op jit(solution)/shard_map/all_gather | solution.py:117
  194.4 8.7 %copy-start.7 = (bf16[1024,512]{0,1:T(8,128)(2,1)S(1)}, bf16[1024,512]{0,1:T(8,128)(2,1)}, u32[]{:S(2)}) copy-start(bf16[1024,512]{0,1:T(8,128)(2,1)} %copy.154) | copy-start | bytes 3145732
  203.1 9.9 %copy-start.4 = (bf16[1,128,4096]{1,2,0:T(8,128)(2,1)S(1)}, bf16[1,128,4096]{1,2,0:T(8,128)(2,1)}, u32[]{:S(2)}) copy-start(bf16[1,128,4096]{1,2,0:T(8,128)(2,1)} %copy.156) | copy-start | bytes 3145732
  236.8 3.5 copy-start.2
  250.2 2.2 copy-start.3
  383.7 33.4 %all-to-all-start.3 = ((bf16[8,2,65536]{2,1,0:T(2,128)(2,1)}), bf16[8,2,65536]{2,1,0:T(2,128)(2,1)}, u32[]{:S(2)}, u32[]{:S(2)}) async-start(bf16[8,2,65536]{2,1,0:T(2,128)(2,1)} %reshape.227), calls=%async_computation.3 | async-start | bytes 4194304 | tf_op jit(solution)/shard_map/all_to_all | solution.py:130
  388.1 357.9 %all-gather.13.cloned.1.call-start = ((), (), s32[]{:S(2)}) async-start(), calls=%async_computation.9 | async-start | bytes 4227072 | tf_op jit(solution)/shard_map/all_gather | solution.py:11
  432.2 2.6 copy-start
  432.2 3.2 copy-start.5
  433.2 7.7 copy-start.1
  442.9 370.1 %reduce-scatter.2.cloned.1.call-start = ((), (), s32[]{:S(2)}) async-start(), calls=%async_computation.8 | async-start | bytes 4456448 | tf_op jit(solution)/shard_map/reduce_scatter | solution.py:120
  442.9 3.5 copy-start.10
Sparse Core Ops, SparseCore 0:
  9.7 54.6 all-gather.6
  127.7 50.8 all-gather.8
  307.8 56.3 all-gather.10
  443.0 303.0 all-gather.12
  748.9 64.0 reduce-scatter.1
